TPU v7x, 32 devices: a whole 2x2x4 slice. The times are simulated.
32 devices in a mesh: vox: 16 (over z, x, core), subj: 2 (over y).
Axes of the slice: x: 2, y: 2, z: 4, core: 2. Of those that a mesh axis runs over, the one named last changes fastest.
Arguments:
- series: bfloat16 [8, 4096, 512], P('subj', 'vox'), may hold values from -6 to 6
- live_mask: int32 [4096], P('vox'), may hold values from 0 to 1, as said below
- neighbours: int32 [4096, 13], P('vox'), may hold values from -1 to 510, as said below
- start_vectors: float32 [4096, 64], P('vox'), may hold values from -60 to 60
Outputs:
- embedding: float32 [4096, 64], P('vox')
Inputs may be any that keep to these rules, and one draw needn't show every extreme that they name: `live_mask`: within each aligned block of 128 voxel slots the live slots are a leading run of 1 to 128 slots. `neighbours`: slot n of voxel i names voxel (i // 256 - 1) * 256 + n, which is live and lies before i; the entries of a row are distinct or -1; rows of dead voxels are all -1; rows of the first 256 voxels name no slot under 256.
All inputs are finite; a program needn't handle non-finite values.
Results may differ from a plain program's by a relative error of at most 0.0024.
Values may be sent and summed in bfloat16 or wider, within the bound.
No kernel may reach another device: no remote copies, remote signals or barrier semaphores. Data moves between devices by JAX's collectives and lax.ppermute only.
A program may use at most 64 MiB of HBM per device.

v0:
```python
import math
import jax
import jax.numpy as jnp
from jax import lax
from jax.sharding import PartitionSpec as P

ITERS = 3


def shifted(shard, axis, by):
    count = lax.axis_size(axis)
    pairs = [(i, i + by) for i in range(count) if 0 <= i + by < count]
    return lax.ppermute(shard, axis, pairs)


def as_sent(shard):
    return jax.tree.map(lambda a: a.astype(jnp.bfloat16) if a.dtype == jnp.float32 else a, shard)


def standard(block):
    values = block.astype(jnp.float32)
    center = values - jnp.mean(values, axis=-1, keepdims=True)
    spread = jnp.mean(center * center, axis=-1, keepdims=True)
    return (center * lax.rsqrt(spread + 1e-05)).astype(jnp.bfloat16)


def orthonormal(images):
    gram_matrix = jnp.dot(images.T, images, precision=lax.Precision.HIGHEST)
    gram_matrix = lax.psum(gram_matrix, "vox")
    factor = jnp.linalg.cholesky(gram_matrix)
    return lax.linalg.triangular_solve(
        factor, images, left_side=False, lower=True, transpose_a=True
    )


def dense_graph(weight, slots, columns_total):
    column_ids = jnp.arange(columns_total, dtype=jnp.int32)
    matrix = jnp.zeros((weight.shape[0], columns_total), jnp.float32)
    for offset in range(weight.shape[1]):
        hits = (slots[:, offset][:, None] == column_ids[None, :]).astype(jnp.float32)
        matrix = matrix + weight[:, offset][:, None] * hits
    return matrix


def product(left, right):
    return jnp.dot(left, right, precision=lax.Precision.HIGHEST)


def on_device(series, live_mask, neighbours, start_vectors):
    voxels_here = series.shape[1]
    frames = series.shape[2]
    subjects = series.shape[0] * lax.axis_size("subj")
    scale_factor = 0.5 / math.sqrt(frames * subjects)
    zscored = standard(series)
    earlier = shifted(zscored, "vox", 1)
    window = jnp.concatenate([earlier, zscored], axis=1)
    present = neighbours >= 0
    safe_slots = jnp.maximum(neighbours, 0)
    columns = []
    for offset in range(neighbours.shape[1]):
        picked = jnp.take(window, safe_slots[:, offset], axis=1)
        columns.append(
            jnp.einsum("svf,svf->v", zscored, picked, preferred_element_type=jnp.float32)
        )
    partial_sums = jnp.stack(columns, axis=1)
    summed = lax.psum(partial_sums, "subj")
    weight = jnp.where(present, jnp.exp(scale_factor * summed), 0.0)
    living = live_mask.astype(jnp.float32)
    local_graph = dense_graph(weight, neighbours, 2 * voxels_here)
    owed = jnp.sum(local_graph, axis=0)
    received = shifted(owed[:voxels_here], "vox", -1)
    degree = 1.0 + jnp.sum(weight, axis=1) + owed[voxels_here:] + received
    scaling = living * lax.rsqrt(degree)
    vectors = living[:, None] * start_vectors
    for repeat in range(ITERS):
        scaled = scaling[:, None] * vectors
        earlier_rows = shifted(as_sent(scaled), "vox", 1).astype(scaled.dtype)
        window_rows = jnp.concatenate([earlier_rows, scaled], axis=0)
        forward = product(local_graph, window_rows)
        returns = product(local_graph.T, scaled)
        arrived = shifted(as_sent(returns[:voxels_here]), "vox", -1)
        images = 0.5 * (
            vectors + scaling[:, None] * (scaled + forward + returns[voxels_here:] + arrived)
        )
        vectors = orthonormal(images)
    return vectors


def solution(mesh):
    placed = (P("subj", "vox", None), P("vox"), P("vox", None), P("vox", None))
    return jax.shard_map(
        on_device, mesh=mesh, in_specs=placed, out_specs=P("vox", None), check_vma=False
    )
```

profile of v0, /device:TPU:0, one launch (start us, length us, event | category | flops | bytes accessed | tf_op | source)
XLA Modules:
  0.0 326.5 jit_solution(9285607745963571878)
XLA Ops:
  5.0 2.6 collective-permute-start
  11.6 2.5 gather_fusion.3
  14.0 2.5 gather_fusion.2
  16.5 2.5 gather_fusion.1
  21.5 2.5 gather_fusion.12
  31.4 2.5 gather_fusion.8
  33.9 2.5 gather_fusion.7
  36.4 2.7 gather_fusion.6
  39.1 2.5 gather_fusion.5
  41.5 2.5 gather_fusion.4
  44.1 9.5 %fusion.7 = (f32[256]{0:T(256)S(1)}, f32[256]{0:T(256)S(1)}, f32[256]{0:T(256)S(1)}, f32[256]{0:T(256)S(1)}) fusion(bf16[256,4,512]{2,1,0:T(4,128)(2,1)} %gather_fusion.3, pred[256]{0:T(512)(128)(4,1)S(1)} %get-tuple-element.72, bf16[256,4,512]{2,1,0:T(4,128)(2,1)} %gather_fusion.2, pred[256]{0:T(512)(128)(4,1)S(1)} %get-tuple-element.73, ...), kind=kLoop, calls=%fused_computation.35 | loop fusion | flops 11009024 | bytes 5256192 | tf_op jit(solution)/shard_map/svf,svf->v/dot_general | solution.py:63
  53.7 14.7 %fusion.16 = (f32[256]{0:T(256)S(1)}, f32[256]{0:T(256)S(1)}, f32[256]{0:T(256)S(1)}, f32[256]{0:T(256)S(1)}, f32[256]{0:T(256)S(1)}, /*index=5*/f32[256]{0:T(25...) fusion(bf16[256,4,512]{2,1,0:T(4,128)(2,1)S(1)} %copy-done.1, pred[256]{0:T(512)(128)(4,1)S(1)} %get-tuple-element.76, ...), kind=kLoop, calls=%fused_computation.44 | loop fusion | flops 21493504 | bytes 10505472 | tf_op jit(solution)/shard_map/svf,svf->v/dot_general | solution.py:63
  68.5 9.0 %psum.28 = f32[256,13]{0,1:T(8,128)S(1)} all-reduce(f32[256,13]{0,1:T(8,128)S(1)} %stack.55), channel_id=1, replica_groups=mesh['vox'=16,'subj'=2] {'subj'}, use_global_device_ids=true, to_apply=%region_2.0 | all-reduce | flops 3328 | bytes 26624 | tf_op jit(solution)/shard_map/psum | solution.py:66
  79.8 9.8 %collective-permute-done.1 = f32[256]{0:T(256)S(1)} collective-permute-done((f32[256]{0:T(256)S(1)}, f32[256]{0:T(256)S(1)}, u32[]{:S(2)}, u32[]{:S(2)}) %collective-permute-start.1) | collective-permute-done | bytes 1056 | tf_op jit(solution)/shard_map/ppermute | solution.py:13
  89.6 7.1 %collective-permute-start.2 = (bf16[256,64]{0,1:T(8,128)(2,1)S(1)}, bf16[256,64]{0,1:T(8,128)(2,1)S(1)}, u32[]{:S(2)}, u32[]{:S(2)}) collective-permute-start(bf16[256,64]{0,1:T(8,128)(2,1)S(1)} %get-tuple-element.25), channel_id=1, source_target_pairs={{0,2},{2,4},{4,6},{6,8},{8,10},{10,12},{12,14},{14,16},{16,18},{18... | collective-permute-start | bytes 98312 | tf_op jit(solution)/shard_map/ppermute | solution.py:13
  101.1 60.4 %psum.29 = f32[64,64]{0,1:T(8,128)S(1)} all-reduce(f32[64,64]{0,1:T(8,128)S(1)} %fusion.66), channel_id=1, replica_groups=mesh['vox'=16,'subj'=2] {'vox'}, use_global_device_ids=true, to_apply=%region_5.7 | all-reduce | flops 4096 | bytes 32768 | tf_op jit(solution)/shard_map/psum | solution.py:29
  161.6 5.8 %cholesky.59 = f32[64,64]{1,0:T(8,128)S(1)} custom-call(f32[64,64]{1,0:T(8,128)S(1)} %fusion.49), custom_call_target="Cholesky" | custom-call | tf_op jit(solution)/shard_map/jit(cholesky)/cholesky | solution.py:30
  168.8 4.9 %custom-call.7 = f32[1,64,64]{1,2,0:T(8,128)S(1)} custom-call(f32[1,64,64]{2,1,0:T(8,128)S(1)} %fusion.41), custom_call_target="InvertDiagBlocksLowerTriangular" | custom-call | tf_op jit(solution)/shard_map/triangular_solve/custom-call.0 | solution.py:31
  179.7 57.9 %psum.30 = f32[64,64]{0,1:T(8,128)S(1)} all-reduce(f32[64,64]{0,1:T(8,128)S(1)} %fusion.68), channel_id=1, replica_groups=mesh['vox'=16,'subj'=2] {'vox'}, use_global_device_ids=true, to_apply=%region_8.12 | all-reduce | flops 4096 | bytes 32768 | tf_op jit(solution)/shard_map/psum | solution.py:29
  237.6 5.8 %cholesky.70 = f32[64,64]{1,0:T(8,128)S(1)} custom-call(f32[64,64]{1,0:T(8,128)S(1)} %fusion.47), custom_call_target="Cholesky" | custom-call | tf_op jit(solution)/shard_map/jit(cholesky)/cholesky | solution.py:30
  244.8 4.9 %custom-call.8 = f32[1,64,64]{1,2,0:T(8,128)S(1)} custom-call(f32[1,64,64]{2,1,0:T(8,128)S(1)} %fusion.42), custom_call_target="InvertDiagBlocksLowerTriangular" | custom-call | tf_op jit(solution)/shard_map/triangular_solve/custom-call.0 | solution.py:31
  255.7 57.7 %psum.31 = f32[64,64]{0,1:T(8,128)S(1)} all-reduce(f32[64,64]{0,1:T(8,128)S(1)} %fusion.70), channel_id=1, replica_groups=mesh['vox'=16,'subj'=2] {'vox'}, use_global_device_ids=true, to_apply=%region_9.13 | all-reduce | flops 4096 | bytes 32768 | tf_op jit(solution)/shard_map/psum | solution.py:29
  313.6 5.8 %cholesky.81 = f32[64,64]{1,0:T(8,128)S(1)} custom-call(f32[64,64]{1,0:T(8,128)S(1)} %fusion.45), custom_call_target="Cholesky" | custom-call | tf_op jit(solution)/shard_map/jit(cholesky)/cholesky | solution.py:30
  320.7 4.9 %custom-call.9 = f32[1,64,64]{1,2,0:T(8,128)S(1)} custom-call(f32[1,64,64]{2,1,0:T(8,128)S(1)} %fusion.43), custom_call_target="InvertDiagBlocksLowerTriangular" | custom-call | tf_op jit(solution)/shard_map/triangular_solve/custom-call.0 | solution.py:31
  (132 shorter events, 42.2 us)
Async XLA Ops:
  0.0 2.2 copy-start
  2.1 5.5 %copy-start.7 = (s32[256,13]{0,1:T(8,128)S(1)}, s32[256,13]{0,1:T(8,128)}, u32[]{:S(2)}) copy-start(s32[256,13]{0,1:T(8,128)} %param.11) | copy-start | bytes 39940
  5.0 5.2 %collective-permute-start = (bf16[4,256,512]{2,0,1:T(4,128)(2,1)S(1)}, bf16[4,256,512]{2,0,1:T(4,128)(2,1)S(1)}, u32[]{:S(2)}, u32[]{:S(2)}) collective-permute-start(bf16[4,256,512]{2,0,1:T(4,128)(2,1)S(1)} %fusion.3), channel_id=1, source_target_pairs={{0,2},{2,4},{4,6},{6,8},{8,10},{10,12},{12,14},{14,16},{16,18},{18... | collective-permute-start | bytes 3145736 | tf_op jit(solution)/shard_map/ppermute | solution.py:13
  44.0 9.6 %copy-start.1 = (bf16[256,4,512]{2,1,0:T(4,128)(2,1)S(1)}, bf16[256,4,512]{2,1,0:T(4,128)(2,1)}, u32[]{:S(2)}) copy-start(bf16[256,4,512]{2,1,0:T(4,128)(2,1)} %gather_fusion.12) | copy-start | bytes 3145732
  44.0 9.6 %copy-start.2 = (bf16[256,4,512]{2,1,0:T(4,128)(2,1)S(1)}, bf16[256,4,512]{2,1,0:T(4,128)(2,1)}, u32[]{:S(2)}) copy-start(bf16[256,4,512]{2,1,0:T(4,128)(2,1)} %gather_fusion.11) | copy-start | bytes 3145732
  44.0 9.6 %copy-start.3 = (bf16[256,4,512]{2,1,0:T(4,128)(2,1)S(1)}, bf16[256,4,512]{2,1,0:T(4,128)(2,1)}, u32[]{:S(2)}) copy-start(bf16[256,4,512]{2,1,0:T(4,128)(2,1)} %gather_fusion.10) | copy-start | bytes 3145732
  44.0 9.6 %copy-start.4 = (bf16[256,4,512]{2,1,0:T(4,128)(2,1)S(1)}, bf16[256,4,512]{2,1,0:T(4,128)(2,1)}, u32[]{:S(2)}) copy-start(bf16[256,4,512]{2,1,0:T(4,128)(2,1)} %gather_fusion.9) | copy-start | bytes 3145732
  44.0 9.6 %copy-start.5 = (bf16[256,4,512]{2,1,0:T(4,128)(2,1)S(1)}, bf16[256,4,512]{2,1,0:T(4,128)(2,1)}, u32[]{:S(2)}) copy-start(bf16[256,4,512]{2,1,0:T(4,128)(2,1)} %gather_fusion.8) | copy-start | bytes 3145732
  44.0 9.6 %copy-start.9 = (pred[256]{0:T(512)(128)(4,1)S(1)}, pred[256]{0:T(512)(128)(4,1)}, u32[]{:S(2)}) copy-start(pred[256]{0:T(512)(128)(4,1)} %get-tuple-element.78) | copy-start | bytes 772
  44.0 9.6 %copy-start.10 = (pred[256]{0:T(512)(128)(4,1)S(1)}, pred[256]{0:T(512)(128)(4,1)}, u32[]{:S(2)}) copy-start(pred[256]{0:T(512)(128)(4,1)} %get-tuple-element.79) | copy-start | bytes 772
  44.0 9.6 %copy-start.11 = (pred[256]{0:T(512)(128)(4,1)S(1)}, pred[256]{0:T(512)(128)(4,1)}, u32[]{:S(2)}) copy-start(pred[256]{0:T(512)(128)(4,1)} %get-tuple-element.80) | copy-start | bytes 772
  44.1 9.6 %copy-start.12 = (pred[256]{0:T(512)(128)(4,1)S(1)}, pred[256]{0:T(512)(128)(4,1)}, u32[]{:S(2)}) copy-start(pred[256]{0:T(512)(128)(4,1)} %get-tuple-element.81) | copy-start | bytes 772
  44.1 9.6 %copy-start.13 = (pred[256]{0:T(512)(128)(4,1)S(1)}, pred[256]{0:T(512)(128)(4,1)}, u32[]{:S(2)}) copy-start(pred[256]{0:T(512)(128)(4,1)} %get-tuple-element.82) | copy-start | bytes 772
  44.1 9.6 %copy-start.14 = (pred[256]{0:T(512)(128)(4,1)S(1)}, pred[256]{0:T(512)(128)(4,1)}, u32[]{:S(2)}) copy-start(pred[256]{0:T(512)(128)(4,1)} %get-tuple-element.83) | copy-start | bytes 772
  44.1 9.6 %copy-start.15 = (pred[256]{0:T(512)(128)(4,1)S(1)}, pred[256]{0:T(512)(128)(4,1)}, u32[]{:S(2)}) copy-start(pred[256]{0:T(512)(128)(4,1)} %compare_and_fusion.8) | copy-start | bytes 772
  53.7 26.1 %copy-start.8 = (s32[256]{0:T(256)S(1)}, s32[256]{0:T(256)}, u32[]{:S(2)}) copy-start(s32[256]{0:T(256)} %param.10) | copy-start | bytes 3076
  53.7 35.9 %copy-start.6 = (f32[256,64]{0,1:T(8,128)S(1)}, f32[256,64]{0,1:T(8,128)}, u32[]{:S(2)}) copy-start(f32[256,64]{0,1:T(8,128)} %param.12) | copy-start | bytes 196612
  78.5 11.1 %collective-permute-start.1 = (f32[256]{0:T(256)S(1)}, f32[256]{0:T(256)S(1)}, u32[]{:S(2)}, u32[]{:S(2)}) collective-permute-start(f32[256]{0:T(256)S(1)} %slice.190), channel_id=1, source_target_pairs={{2,0},{4,2},{6,4},{8,6},{10,8},{12,10},{14,12},{16,14},{18,16},{20... | collective-permute-start | bytes 3080 | tf_op jit(solution)/shard_map/ppermute | solution.py:13
  89.6 8.8 %collective-permute-start.2 = (bf16[256,64]{0,1:T(8,128)(2,1)S(1)}, bf16[256,64]{0,1:T(8,128)(2,1)S(1)}, u32[]{:S(2)}, u32[]{:S(2)}) collective-permute-start(bf16[256,64]{0,1:T(8,128)(2,1)S(1)} %get-tuple-element.25), channel_id=1, source_target_pairs={{0,2},{2,4},{4,6},{6,8},{8,10},{10,12},{12,14},{14,16},{16,18},{18... | collective-permute-start | bytes 98312 | tf_op jit(solution)/shard_map/ppermute | solution.py:13
  97.1 3.1 collective-permute-start.3
  174.0 3.1 collective-permute-start.4
  175.7 3.1 collective-permute-start.5
  250.0 3.1 collective-permute-start.6
  251.8 3.1 collective-permute-start.7
where the time goes:
time: 327 us
  blocking collectives  185 us (57%)
  other arithmetic  70 us (21%)
  local copies, waits for them, and re-layouts  32.8 us (10%)
  starting transfers between devices  17.5 us (5%)
  waiting for transfers between devices  15.1 us (5%)
  matrix products  5.26 us (2%)
    psum x3, blocking collectives, orthonormal(): gram_matrix = lax.psum(gram_matrix, 'vox')  176 us
    gather x13, local copies, waits for them, and re-layouts, on_device(): picked = jnp.take(window, safe_slots[:, offset], axis=1)  32.4 us
    dot_general x2, other arithmetic, on_device(): jnp.einsum('svf,svf->v', zscored, picked, preferred_element_type=jnp.floa...  24.1 us
    another operation x9, other arithmetic, orthonormal(): factor = jnp.linalg.cholesky(gram_matrix)  19.6 us
    ppermute x8, starting transfers between devices, shifted(): return lax.ppermute(shard, axis, pairs)  17.5 us
    another operation x6, other arithmetic, orthonormal(): lax.linalg.triangular_solve(factor, images, left_side=False, lower=True,...  16.6 us
    ppermute x8, waiting for transfers between devices, shifted(): return lax.ppermute(shard, axis, pairs)  15.1 us
    psum x1, blocking collectives, on_device(): summed = lax.psum(partial_sums, 'subj')  8.99 us
  transfers between devices with their start and end apart: 8, of which 4 were waited for; matrix products, arithmetic and copies ran while one was open for 1% of the time, Pallas kernels for 0%

commit v1 on v0

--- a/solution.py
+++ b/solution.py
@@ -26,7 +26,7 @@
 
 def orthonormal(images):
     gram_matrix = jnp.dot(images.T, images, precision=lax.Precision.HIGHEST)
-    gram_matrix = lax.psum(gram_matrix, "vox")
+    gram_matrix = jnp.sum(lax.all_gather(gram_matrix, "vox"), axis=0)
     factor = jnp.linalg.cholesky(gram_matrix)
     return lax.linalg.triangular_solve(
         factor, images, left_side=False, lower=True, transpose_a=True

time: 327 us -> 219 us (0.67)
  blocking collectives: 185 us -> 74.8 us
    psum x3 -> x0, blocking collectives: 176 us -> none  [orthonormal(): gram_matrix = lax.psum(gram_matrix, 'vox')]
    all_gather x0 -> x3, blocking collectives: none -> 65.8 us  [orthonormal(): gram_matrix = jnp.sum(lax.all_gather(gram_matrix, 'vox'), axis=0)]
  transfers between devices with their start and end apart: 8 -> 8, of which waited for: 4 -> 4; matrix products, arithmetic and copies ran while one was open for 1% -> 2% of each run, Pallas kernels for 0% -> 0%
where the time goes in v1:
time: 219 us; the launch traced here: 218 us
  blocking collectives  74.8 us (34%)
  other arithmetic  70.2 us (32%)
  local copies, waits for them, and re-layouts  32.8 us (15%)
  starting transfers between devices  19.4 us (9%)
  waiting for transfers between devices  15.1 us (7%)
  matrix products  5.26 us (2%)
    all_gather x3, blocking collectives, orthonormal(): gram_matrix = jnp.sum(lax.all_gather(gram_matrix, 'vox'), axis=0)  65.8 us
    gather x13, local copies, waits for them, and re-layouts, on_device(): picked = jnp.take(window, safe_slots[:, offset], axis=1)  32.4 us
    dot_general x2, other arithmetic, on_device(): jnp.einsum('svf,svf->v', zscored, picked, preferred_element_type=jnp.floa...  24.1 us
    another operation x9, other arithmetic, orthonormal(): factor = jnp.linalg.cholesky(gram_matrix)  19.6 us
    ppermute x8, starting transfers between devices, shifted(): return lax.ppermute(shard, axis, pairs)  19.4 us
    another operation x6, other arithmetic, orthonormal(): lax.linalg.triangular_solve(factor, images, left_side=False, lower=True,...  16.6 us
    ppermute x8, waiting for transfers between devices, shifted(): return lax.ppermute(shard, axis, pairs)  15.1 us
    psum x1, blocking collectives, on_device(): summed = lax.psum(partial_sums, 'subj')  8.99 us
  transfers between devices with their start and end apart: 8, of which 4 were waited for; matrix products, arithmetic and copies ran while one was open for 2% of the time, Pallas kernels for 0%

profile of v1, /device:TPU:0, one launch (start us, length us, event | category | flops | bytes accessed | tf_op | source)
XLA Modules:
  0.0 218.3 jit_solution(9593848405151555083)
XLA Ops:
  5.0 2.6 %collective-permute-start = (bf16[4,256,512]{2,0,1:T(4,128)(2,1)S(1)}, bf16[4,256,512]{2,0,1:T(4,128)(2,1)S(1)}, u32[]{:S(2)}, u32[]{:S(2)}) collective-permute-start(bf16[4,256,512]{2,0,1:T(4,128)(2,1)S(1)} %fusion.3), channel_id=1, source_target_pairs={{0,2},{2,4},{4,6},{6,8},{8,10},{10,12},{12,14},{14,16},{16,18},{18... | collective-permute-start | bytes 3145736 | tf_op jit(solution)/shard_map/ppermute | solution.py:13
  11.6 2.5 %gather_fusion.3 = bf16[256,4,512]{2,1,0:T(4,128)(2,1)} fusion(bf16[4,512,512]{2,0,1:T(4,128)(2,1)S(1)} %pad_maximum_fusion, s32[1024]{0:T(1024)S(1)} %pad_clamp_fusion.9), kind=kCustom, calls=%fused_computation.3.clone | custom fusion | bytes 2098176 | tf_op jit(solution)/shard_map/jit(_take)/gather | solution.py:61
  14.0 2.5 %gather_fusion.2 = bf16[256,4,512]{2,1,0:T(4,128)(2,1)} fusion(bf16[4,512,512]{2,0,1:T(4,128)(2,1)S(1)} %pad_maximum_fusion, s32[1024]{0:T(1024)S(1)} %pad_clamp_fusion.10), kind=kCustom, calls=%fused_computation.2.clone | custom fusion | bytes 2098176 | tf_op jit(solution)/shard_map/jit(_take)/gather | solution.py:61
  16.5 2.5 %gather_fusion.1 = bf16[256,4,512]{2,1,0:T(4,128)(2,1)} fusion(bf16[4,512,512]{2,0,1:T(4,128)(2,1)S(1)} %pad_maximum_fusion, s32[1024]{0:T(1024)S(1)} %pad_clamp_fusion.11), kind=kCustom, calls=%fused_computation.1.clone | custom fusion | bytes 2098176 | tf_op jit(solution)/shard_map/jit(_take)/gather | solution.py:61
  21.5 2.5 %gather_fusion.12 = bf16[256,4,512]{2,1,0:T(4,128)(2,1)} fusion(bf16[4,512,512]{2,0,1:T(4,128)(2,1)S(1)} %pad_maximum_fusion, s32[1024]{0:T(1024)S(1)} %pad_clamp_fusion), kind=kCustom, calls=%fused_computation.12.clone | custom fusion | bytes 2098176 | tf_op jit(solution)/shard_map/jit(_take)/gather | solution.py:61
  31.4 2.5 %gather_fusion.8 = bf16[256,4,512]{2,1,0:T(4,128)(2,1)} fusion(bf16[4,512,512]{2,0,1:T(4,128)(2,1)S(1)} %pad_maximum_fusion, s32[1024]{0:T(1024)S(1)} %pad_clamp_fusion.4), kind=kCustom, calls=%fused_computation.8.clone | custom fusion | bytes 2098176 | tf_op jit(solution)/shard_map/jit(_take)/gather | solution.py:61
  33.9 2.5 %gather_fusion.7 = bf16[256,4,512]{2,1,0:T(4,128)(2,1)} fusion(bf16[4,512,512]{2,0,1:T(4,128)(2,1)S(1)} %pad_maximum_fusion, s32[1024]{0:T(1024)S(1)} %pad_clamp_fusion.5), kind=kCustom, calls=%fused_computation.7.clone | custom fusion | bytes 2098176 | tf_op jit(solution)/shard_map/jit(_take)/gather | solution.py:61
  36.4 2.7 %gather_fusion.6 = bf16[256,4,512]{2,1,0:T(4,128)(2,1)} fusion(bf16[4,512,512]{2,0,1:T(4,128)(2,1)S(1)} %pad_maximum_fusion, s32[1024]{0:T(1024)S(1)} %pad_clamp_fusion.6), kind=kCustom, calls=%fused_computation.6.clone | custom fusion | bytes 2098176 | tf_op jit(solution)/shard_map/jit(_take)/gather | solution.py:61
  39.1 2.5 %gather_fusion.5 = bf16[256,4,512]{2,1,0:T(4,128)(2,1)} fusion(bf16[4,512,512]{2,0,1:T(4,128)(2,1)S(1)} %pad_maximum_fusion, s32[1024]{0:T(1024)S(1)} %pad_clamp_fusion.7), kind=kCustom, calls=%fused_computation.5.clone | custom fusion | bytes 2098176 | tf_op jit(solution)/shard_map/jit(_take)/gather | solution.py:61
  41.5 2.5 %gather_fusion.4 = bf16[256,4,512]{2,1,0:T(4,128)(2,1)} fusion(bf16[4,512,512]{2,0,1:T(4,128)(2,1)S(1)} %pad_maximum_fusion, s32[1024]{0:T(1024)S(1)} %pad_clamp_fusion.8), kind=kCustom, calls=%fused_computation.4.clone | custom fusion | bytes 2098176 | tf_op jit(solution)/shard_map/jit(_take)/gather | solution.py:61
  44.1 9.5 %fusion.7 = (f32[256]{0:T(256)S(1)}, f32[256]{0:T(256)S(1)}, f32[256]{0:T(256)S(1)}, f32[256]{0:T(256)S(1)}) fusion(bf16[256,4,512]{2,1,0:T(4,128)(2,1)} %gather_fusion.3, pred[256]{0:T(512)(128)(4,1)S(1)} %get-tuple-element.72, bf16[256,4,512]{2,1,0:T(4,128)(2,1)} %gather_fusion.2, pred[256]{0:T(512)(128)(4,1)S(1)} %get-tuple-element.73, ...), kind=kLoop, calls=%fused_computation.35 | loop fusion | flops 11009024 | bytes 5256192 | tf_op jit(solution)/shard_map/svf,svf->v/dot_general | solution.py:63
  53.7 14.7 %fusion.16 = (f32[256]{0:T(256)S(1)}, f32[256]{0:T(256)S(1)}, f32[256]{0:T(256)S(1)}, f32[256]{0:T(256)S(1)}, f32[256]{0:T(256)S(1)}, /*index=5*/f32[256]{0:T(25...) fusion(bf16[256,4,512]{2,1,0:T(4,128)(2,1)S(1)} %copy-done.1, pred[256]{0:T(512)(128)(4,1)S(1)} %get-tuple-element.76, ...), kind=kLoop, calls=%fused_computation.44 | loop fusion | flops 21493504 | bytes 10505472 | tf_op jit(solution)/shard_map/svf,svf->v/dot_general | solution.py:63
  68.5 9.0 %psum.7 = f32[256,13]{0,1:T(8,128)S(1)} all-reduce(f32[256,13]{0,1:T(8,128)S(1)} %stack.55), channel_id=1, replica_groups=mesh['vox'=16,'subj'=2] {'subj'}, use_global_device_ids=true, to_apply=%region_2.0 | all-reduce | flops 3328 | bytes 26624 | tf_op jit(solution)/shard_map/psum | solution.py:66
  79.8 9.8 %collective-permute-done.1 = f32[256]{0:T(256)S(1)} collective-permute-done((f32[256]{0:T(256)S(1)}, f32[256]{0:T(256)S(1)}, u32[]{:S(2)}, u32[]{:S(2)}) %collective-permute-start.1) | collective-permute-done | bytes 1056 | tf_op jit(solution)/shard_map/ppermute | solution.py:13
  89.6 7.1 %collective-permute-start.2 = (bf16[256,64]{0,1:T(8,128)(2,1)S(1)}, bf16[256,64]{0,1:T(8,128)(2,1)S(1)}, u32[]{:S(2)}, u32[]{:S(2)}) collective-permute-start(bf16[256,64]{0,1:T(8,128)(2,1)S(1)} %get-tuple-element.25), channel_id=1, source_target_pairs={{0,2},{2,4},{4,6},{6,8},{8,10},{10,12},{12,14},{14,16},{16,18},{18... | collective-permute-start | bytes 98312 | tf_op jit(solution)/shard_map/ppermute | solution.py:13
  101.1 23.6 %all-gather = f32[1024,64]{1,0:T(8,128)S(1)} all-gather(f32[64,64]{1,0:T(8,128)S(1)} %fusion.66), channel_id=2, replica_groups=mesh['vox'=16,'subj'=2] {'vox'}, dimensions={0}, use_global_device_ids=true | all-gather | bytes 278528 | tf_op jit(solution)/shard_map/all_gather | solution.py:29
  124.9 5.8 %cholesky.59 = f32[64,64]{1,0:T(8,128)S(1)} custom-call(f32[64,64]{1,0:T(8,128)S(1)} %fusion.49), custom_call_target="Cholesky" | custom-call | tf_op jit(solution)/shard_map/jit(cholesky)/cholesky | solution.py:30
  132.1 4.9 %custom-call.7 = f32[1,64,64]{1,2,0:T(8,128)S(1)} custom-call(f32[1,64,64]{2,1,0:T(8,128)S(1)} %fusion.41), custom_call_target="InvertDiagBlocksLowerTriangular" | custom-call | tf_op jit(solution)/shard_map/triangular_solve/custom-call.0 | solution.py:31
  143.9 21.2 %all-gather.1 = f32[1024,64]{1,0:T(8,128)S(1)} all-gather(f32[64,64]{1,0:T(8,128)S(1)} %fusion.68), channel_id=3, replica_groups=mesh['vox'=16,'subj'=2] {'vox'}, dimensions={0}, use_global_device_ids=true | all-gather | bytes 278528 | tf_op jit(solution)/shard_map/all_gather | solution.py:29
  165.3 5.8 %cholesky.70 = f32[64,64]{1,0:T(8,128)S(1)} custom-call(f32[64,64]{1,0:T(8,128)S(1)} %fusion.47), custom_call_target="Cholesky" | custom-call | tf_op jit(solution)/shard_map/jit(cholesky)/cholesky | solution.py:30
  172.4 4.9 %custom-call.8 = f32[1,64,64]{1,2,0:T(8,128)S(1)} custom-call(f32[1,64,64]{2,1,0:T(8,128)S(1)} %fusion.42), custom_call_target="InvertDiagBlocksLowerTriangular" | custom-call | tf_op jit(solution)/shard_map/triangular_solve/custom-call.0 | solution.py:31
  184.3 20.9 %all-gather.2 = f32[1024,64]{1,0:T(8,128)S(1)} all-gather(f32[64,64]{1,0:T(8,128)S(1)} %fusion.70), channel_id=4, replica_groups=mesh['vox'=16,'subj'=2] {'vox'}, dimensions={0}, use_global_device_ids=true | all-gather | bytes 278528 | tf_op jit(solution)/shard_map/all_gather | solution.py:29
  205.4 5.8 %cholesky.81 = f32[64,64]{1,0:T(8,128)S(1)} custom-call(f32[64,64]{1,0:T(8,128)S(1)} %fusion.45), custom_call_target="Cholesky" | custom-call | tf_op jit(solution)/shard_map/jit(cholesky)/cholesky | solution.py:30
  212.5 4.9 %custom-call.9 = f32[1,64,64]{1,2,0:T(8,128)S(1)} custom-call(f32[1,64,64]{2,1,0:T(8,128)S(1)} %fusion.43), custom_call_target="InvertDiagBlocksLowerTriangular" | custom-call | tf_op jit(solution)/shard_map/triangular_solve/custom-call.0 | solution.py:31
  (135 shorter events, 44.3 us)
Async XLA Ops:
  0.0 2.2 copy-start
  2.1 5.5 %copy-start.7 = (s32[256,13]{0,1:T(8,128)S(1)}, s32[256,13]{0,1:T(8,128)}, u32[]{:S(2)}) copy-start(s32[256,13]{0,1:T(8,128)} %param.11) | copy-start | bytes 39940
  5.0 5.2 %collective-permute-start = (bf16[4,256,512]{2,0,1:T(4,128)(2,1)S(1)}, bf16[4,256,512]{2,0,1:T(4,128)(2,1)S(1)}, u32[]{:S(2)}, u32[]{:S(2)}) collective-permute-start(bf16[4,256,512]{2,0,1:T(4,128)(2,1)S(1)} %fusion.3), channel_id=1, source_target_pairs={{0,2},{2,4},{4,6},{6,8},{8,10},{10,12},{12,14},{14,16},{16,18},{18... | collective-permute-start | bytes 3145736 | tf_op jit(solution)/shard_map/ppermute | solution.py:13
  44.0 9.6 %copy-start.1 = (bf16[256,4,512]{2,1,0:T(4,128)(2,1)S(1)}, bf16[256,4,512]{2,1,0:T(4,128)(2,1)}, u32[]{:S(2)}) copy-start(bf16[256,4,512]{2,1,0:T(4,128)(2,1)} %gather_fusion.12) | copy-start | bytes 3145732
  44.0 9.6 %copy-start.2 = (bf16[256,4,512]{2,1,0:T(4,128)(2,1)S(1)}, bf16[256,4,512]{2,1,0:T(4,128)(2,1)}, u32[]{:S(2)}) copy-start(bf16[256,4,512]{2,1,0:T(4,128)(2,1)} %gather_fusion.11) | copy-start | bytes 3145732
  44.0 9.6 %copy-start.3 = (bf16[256,4,512]{2,1,0:T(4,128)(2,1)S(1)}, bf16[256,4,512]{2,1,0:T(4,128)(2,1)}, u32[]{:S(2)}) copy-start(bf16[256,4,512]{2,1,0:T(4,128)(2,1)} %gather_fusion.10) | copy-start | bytes 3145732
  44.0 9.6 %copy-start.4 = (bf16[256,4,512]{2,1,0:T(4,128)(2,1)S(1)}, bf16[256,4,512]{2,1,0:T(4,128)(2,1)}, u32[]{:S(2)}) copy-start(bf16[256,4,512]{2,1,0:T(4,128)(2,1)} %gather_fusion.9) | copy-start | bytes 3145732
  44.0 9.6 %copy-start.5 = (bf16[256,4,512]{2,1,0:T(4,128)(2,1)S(1)}, bf16[256,4,512]{2,1,0:T(4,128)(2,1)}, u32[]{:S(2)}) copy-start(bf16[256,4,512]{2,1,0:T(4,128)(2,1)} %gather_fusion.8) | copy-start | bytes 3145732
  44.0 9.6 %copy-start.9 = (pred[256]{0:T(512)(128)(4,1)S(1)}, pred[256]{0:T(512)(128)(4,1)}, u32[]{:S(2)}) copy-start(pred[256]{0:T(512)(128)(4,1)} %get-tuple-element.78) | copy-start | bytes 772
  44.0 9.6 %copy-start.10 = (pred[256]{0:T(512)(128)(4,1)S(1)}, pred[256]{0:T(512)(128)(4,1)}, u32[]{:S(2)}) copy-start(pred[256]{0:T(512)(128)(4,1)} %get-tuple-element.79) | copy-start | bytes 772
  44.0 9.6 %copy-start.11 = (pred[256]{0:T(512)(128)(4,1)S(1)}, pred[256]{0:T(512)(128)(4,1)}, u32[]{:S(2)}) copy-start(pred[256]{0:T(512)(128)(4,1)} %get-tuple-element.80) | copy-start | bytes 772
  44.1 9.6 %copy-start.12 = (pred[256]{0:T(512)(128)(4,1)S(1)}, pred[256]{0:T(512)(128)(4,1)}, u32[]{:S(2)}) copy-start(pred[256]{0:T(512)(128)(4,1)} %get-tuple-element.81) | copy-start | bytes 772
  44.1 9.6 %copy-start.13 = (pred[256]{0:T(512)(128)(4,1)S(1)}, pred[256]{0:T(512)(128)(4,1)}, u32[]{:S(2)}) copy-start(pred[256]{0:T(512)(128)(4,1)} %get-tuple-element.82) | copy-start | bytes 772
  44.1 9.6 %copy-start.14 = (pred[256]{0:T(512)(128)(4,1)S(1)}, pred[256]{0:T(512)(128)(4,1)}, u32[]{:S(2)}) copy-start(pred[256]{0:T(512)(128)(4,1)} %get-tuple-element.83) | copy-start | bytes 772
  44.1 9.6 %copy-start.15 = (pred[256]{0:T(512)(128)(4,1)S(1)}, pred[256]{0:T(512)(128)(4,1)}, u32[]{:S(2)}) copy-start(pred[256]{0:T(512)(128)(4,1)} %compare_and_fusion.8) | copy-start | bytes 772
  53.7 26.1 %copy-start.8 = (s32[256]{0:T(256)S(1)}, s32[256]{0:T(256)}, u32[]{:S(2)}) copy-start(s32[256]{0:T(256)} %param.10) | copy-start | bytes 3076
  53.7 35.9 %copy-start.6 = (f32[256,64]{0,1:T(8,128)S(1)}, f32[256,64]{0,1:T(8,128)}, u32[]{:S(2)}) copy-start(f32[256,64]{0,1:T(8,128)} %param.12) | copy-start | bytes 196612
  78.5 11.1 %collective-permute-start.1 = (f32[256]{0:T(256)S(1)}, f32[256]{0:T(256)S(1)}, u32[]{:S(2)}, u32[]{:S(2)}) collective-permute-start(f32[256]{0:T(256)S(1)} %slice.190), channel_id=1, source_target_pairs={{2,0},{4,2},{6,4},{8,6},{10,8},{12,10},{14,12},{16,14},{18,16},{20... | collective-permute-start | bytes 3080 | tf_op jit(solution)/shard_map/ppermute | solution.py:13
  89.6 8.8 %collective-permute-start.2 = (bf16[256,64]{0,1:T(8,128)(2,1)S(1)}, bf16[256,64]{0,1:T(8,128)(2,1)S(1)}, u32[]{:S(2)}, u32[]{:S(2)}) collective-permute-start(bf16[256,64]{0,1:T(8,128)(2,1)S(1)} %get-tuple-element.25), channel_id=1, source_target_pairs={{0,2},{2,4},{4,6},{6,8},{8,10},{10,12},{12,14},{14,16},{16,18},{18... | collective-permute-start | bytes 98312 | tf_op jit(solution)/shard_map/ppermute | solution.py:13
  97.1 3.1 %collective-permute-start.3 = (bf16[256,64]{0,1:T(8,128)(2,1)S(1)}, bf16[256,64]{0,1:T(8,128)(2,1)S(1)}, u32[]{:S(2)}, u32[]{:S(2)}) collective-permute-start(bf16[256,64]{0,1:T(8,128)(2,1)S(1)} %slice.264), channel_id=1, source_target_pairs={{2,0},{4,2},{6,4},{8,6},{10,8},{12,10},{14,12},{16,14},{18,16},{20... | collective-permute-start | bytes 98312 | tf_op jit(solution)/shard_map/ppermute | solution.py:13
  137.2 4.0 %collective-permute-start.4 = (bf16[256,64]{0,1:T(8,128)(2,1)S(1)}, bf16[256,64]{0,1:T(8,128)(2,1)S(1)}, u32[]{:S(2)}, u32[]{:S(2)}) collective-permute-start(bf16[256,64]{0,1:T(8,128)(2,1)S(1)} %get-tuple-element.23), channel_id=1, source_target_pairs={{0,2},{2,4},{4,6},{6,8},{8,10},{10,12},{12,14},{14,16},{16,18},{18... | collective-permute-start | bytes 98312 | tf_op jit(solution)/shard_map/ppermute | solution.py:13
  140.0 3.1 %collective-permute-start.5 = (bf16[256,64]{0,1:T(8,128)(2,1)S(1)}, bf16[256,64]{0,1:T(8,128)(2,1)S(1)}, u32[]{:S(2)}, u32[]{:S(2)}) collective-permute-start(bf16[256,64]{0,1:T(8,128)(2,1)S(1)} %slice.263), channel_id=1, source_target_pairs={{2,0},{4,2},{6,4},{8,6},{10,8},{12,10},{14,12},{16,14},{18,16},{20... | collective-permute-start | bytes 98312 | tf_op jit(solution)/shard_map/ppermute | solution.py:13
  177.6 4.0 %collective-permute-start.6 = (bf16[256,64]{0,1:T(8,128)(2,1)S(1)}, bf16[256,64]{0,1:T(8,128)(2,1)S(1)}, u32[]{:S(2)}, u32[]{:S(2)}) collective-permute-start(bf16[256,64]{0,1:T(8,128)(2,1)S(1)} %get-tuple-element.21), channel_id=1, source_target_pairs={{0,2},{2,4},{4,6},{6,8},{8,10},{10,12},{12,14},{14,16},{16,18},{18... | collective-permute-start | bytes 98312 | tf_op jit(solution)/shard_map/ppermute | solution.py:13
  180.4 3.1 %collective-permute-start.7 = (bf16[256,64]{0,1:T(8,128)(2,1)S(1)}, bf16[256,64]{0,1:T(8,128)(2,1)S(1)}, u32[]{:S(2)}, u32[]{:S(2)}) collective-permute-start(bf16[256,64]{0,1:T(8,128)(2,1)S(1)} %slice.262), channel_id=1, source_target_pairs={{2,0},{4,2},{6,4},{8,6},{10,8},{12,10},{14,12},{16,14},{18,16},{20... | collective-permute-start | bytes 98312 | tf_op jit(solution)/shard_map/ppermute | solution.py:13
